TPU v7x, 256 devices: a whole 4x4x8 slice. The times are simulated.
256 devices in a mesh: grp: 8 (over y, core), chan: 32 (over z, x).
Axes of the slice: x: 4, y: 4, z: 8, core: 2. Of those that a mesh axis runs over, the one named last changes fastest.
Arguments:
- fibre_records: bfloat16 [2048, 256, 1536], P(('grp', 'chan')), may hold values from -6 to 6
- station_records: bfloat16 [1024, 256, 1536], P('chan'), may hold values from -6 to 6
- band_mask: int32 [8, 256], replicated, may hold values 0 or 1
- station_valid: int32 [1024], P('chan'), may hold values 0 or 1
- segment_keep: int32 [256], replicated, may hold values 0 or 1
Outputs:
- cross_spectra: float32 [2, 8, 2048, 1024], P(None, None, ('grp', 'chan'))
All inputs are finite; a program needn't handle non-finite values. No bound on the sum of `station_valid` on one device may be relied on, other than what follows from the above.
Results may differ from a plain program's by a relative error of at most 0.0072.
Values may be sent and summed in bfloat16 or wider, within the bound.
No kernel may reach another device: no remote copies, remote signals or barrier semaphores. Data moves between devices by JAX's collectives and lax.ppermute only.
A program may use at most 128 MiB of HBM per device.

v0:
```python
import math
import jax
import jax.numpy as jnp
from jax import lax
from jax.sharding import PartitionSpec as P

SEG = 256
SAMPLES = 1536
NFREQ = 8
FIRST_BIN = 24


def laid_out(blocks, dim):
    lengths = list(blocks.shape[1:])
    lengths[dim] *= blocks.shape[0]
    return jnp.moveaxis(blocks, 0, dim).reshape(lengths)


def from_everyone(x, axis):
    copies = jnp.broadcast_to(x, (lax.axis_size(axis), *x.shape))
    return lax.all_to_all(copies, axis, split_axis=0, concat_axis=0, tiled=True)


def collect(x, axis, dim):
    return laid_out(from_everyone(x, axis), dim)


def time_table():
    sample_index = jnp.arange(SAMPLES, dtype=jnp.int32)
    bin_index = FIRST_BIN + jnp.arange(NFREQ, dtype=jnp.int32)
    phase = sample_index[:, None] * bin_index[None, :] % SAMPLES
    angle = phase.astype(jnp.float32) * (2.0 * math.pi / SAMPLES)
    return jnp.concatenate([jnp.cos(angle), -jnp.sin(angle)], axis=1).astype(jnp.bfloat16)


def wave_tables(width):
    index = jnp.arange(width, dtype=jnp.int32)
    phase = index[:, None] * index[None, :] % width
    angle = phase.astype(jnp.float32) * (2.0 * math.pi / width)
    return (jnp.cos(angle).astype(jnp.bfloat16), jnp.sin(angle).astype(jnp.bfloat16))


def matmul(left, right):
    return jnp.dot(left, right, preferred_element_type=jnp.float32)


def wavenumber_filter(spectra, cosines, sines, weights):
    width, count = (spectra.shape[0], spectra.shape[1])
    real_part = spectra[:, :, :NFREQ].reshape(width, count * NFREQ)
    imag_part = spectra[:, :, NFREQ:].reshape(width, count * NFREQ)
    fwd_real = matmul(cosines, real_part) + matmul(sines, imag_part)
    fwd_imag = matmul(cosines, imag_part) - matmul(sines, real_part)
    fwd_real = (
        (fwd_real.reshape(width, count, NFREQ) * weights[:, None, :])
        .astype(jnp.bfloat16)
        .reshape(width, count * NFREQ)
    )
    fwd_imag = (
        (fwd_imag.reshape(width, count, NFREQ) * weights[:, None, :])
        .astype(jnp.bfloat16)
        .reshape(width, count * NFREQ)
    )
    back_real = (matmul(cosines, fwd_real) - matmul(sines, fwd_imag)) / width
    back_imag = (matmul(sines, fwd_real) + matmul(cosines, fwd_imag)) / width
    joined = jnp.concatenate(
        [back_real.reshape(width, count, NFREQ), back_imag.reshape(width, count, NFREQ)], axis=2
    )
    return joined.astype(jnp.bfloat16)


def scale_rows(spectra, totals, valid):
    factor = lax.rsqrt(totals / (2 * SEG * NFREQ) + 1e-06) * valid.astype(jnp.float32)
    return (spectra * factor[:, None, None]).astype(jnp.bfloat16)


def transform(records, dft_table):
    rows, segs = (records.shape[0], records.shape[1])
    return matmul(records.reshape(rows * segs, SAMPLES), dft_table).reshape(rows, segs, 2 * NFREQ)


def pair_spectra(fibre_part, keep_part, band_part):
    kept = fibre_part * keep_part.astype(jnp.bfloat16)[None, :, None]
    fibre_four = kept.reshape(kept.shape[0], kept.shape[1], 2, NFREQ)
    band_four = band_part.reshape(band_part.shape[0], band_part.shape[1], 2, NFREQ)
    rotated = jnp.concatenate([-band_four[:, :, 1:], band_four[:, :, :1]], axis=2)
    real_out = jnp.einsum(
        "cgpb,sgpb->bcs", fibre_four, band_four, preferred_element_type=jnp.float32
    )
    imag_out = jnp.einsum("cgpb,sgpb->bcs", fibre_four, rotated, preferred_element_type=jnp.float32)
    return jnp.stack([real_out, imag_out])


def shards(fibre_records, station_records, band_mask, station_valid, segment_keep):
    dft_table = time_table()
    channels_here = fibre_records.shape[0]
    chan_count = lax.axis_size("chan")
    block_width = channels_here * chan_count
    seg_local = SEG // chan_count
    fibre_spec = transform(fibre_records, dft_table).astype(jnp.bfloat16)
    station_spec = transform(station_records, dft_table)
    totals = jnp.sum(station_spec * station_spec, axis=(1, 2))
    bands_local = scale_rows(station_spec, totals, station_valid)
    cosines, sines = wave_tables(block_width)
    weights = band_mask.T.astype(jnp.float32)
    outgoing = fibre_spec.reshape(channels_here, chan_count, seg_local, 2 * NFREQ)
    arrived = lax.all_to_all(outgoing, "chan", split_axis=1, concat_axis=0, tiled=True)
    width = arrived.shape[0]
    count = arrived.shape[2]
    result = wavenumber_filter(arrived.reshape(width, count, 2 * NFREQ), cosines, sines, weights)
    filtered_block = result.reshape(width, 1, count, 2 * NFREQ)
    filtered_block = filtered_block.reshape(block_width, seg_local, 2 * NFREQ)
    piece = collect(filtered_block, "chan", 1)
    block_cross = pair_spectra(piece, segment_keep, bands_local)
    result = lax.all_to_all(
        block_cross.astype(jnp.bfloat16), "chan", split_axis=2, concat_axis=3, tiled=True
    ).astype(block_cross.dtype)
    return result * (1.0 / math.sqrt(SEG * SAMPLES))


def solution(mesh):
    placed = (P(("grp", "chan"), None, None), P("chan", None, None), P(), P("chan"), P())
    return jax.shard_map(
        shards,
        mesh=mesh,
        in_specs=placed,
        out_specs=P(None, None, ("grp", "chan"), None),
        check_vma=False,
    )
```

profile of v0, /device:TPU:16, one launch (start us, length us, event | category | flops | bytes accessed | tf_op | source)
XLA Modules:
  0.0 125.0 jit_solution(6500059093318800454)
XLA Ops:
  0.3 4.5 %fusion = bf16[2048,16]{0,1:T(8,128)(2,1)S(1)} fusion(bf16[2048,1536]{1,0:T(8,128)(2,1)} %bitcast.79, bf16[1536,8]{0,1:T(8,128)(2,1)S(1)} %get-tuple-element.10, bf16[1536,8]{0,1:T(8,128)(2,1)S(1)} %get-tuple-element.9), kind=kOutput, calls=%fused_computation.1 | convolution fusion | flops 100794368 | bytes 6406144 | tf_op jit(solution)/shard_map/dot_general | solution.py:44
  5.3 1.2 reshape.69
  6.5 11.3 %all-to-all-start = ((bf16[32,2,512]{2,1,0:T(2,128)(2,1)}), bf16[32,2,512]{2,1,0:T(2,128)(2,1)S(1)}, u32[]{:S(2)}, u32[]{:S(2)}) async-start(bf16[32,2,512]{2,1,0:T(2,128)(2,1)} %reshape.69), calls=%async_computation | async-start | bytes 131072 | tf_op jit(solution)/shard_map/all_to_all | solution.py:106
  17.8 9.9 %all-to-all-done = bf16[32,2,512]{2,1,0:T(2,128)(2,1)S(1)} async-done(((bf16[32,2,512]{2,1,0:T(2,128)(2,1)}), bf16[32,2,512]{2,1,0:T(2,128)(2,1)S(1)}, u32[]{:S(2)}, u32[]{:S(2)}) %all-to-all-start) | async-done | bytes 65568 | tf_op jit(solution)/shard_map/all_to_all | solution.py:106
  28.7 1.1 fusion.26
  30.1 1.1 fusion.28
  31.2 1.1 fusion.9
  32.3 1.1 fusion.27
  33.4 1.1 fusion.29
  34.5 1.1 fusion.10
  35.6 1.1 fusion.14
  36.7 1.1 fusion.13
  37.8 1.6 %broadcast_in_dim.2 = bf16[32,256,8,16]{1,3,2,0:T(8,128)(2,1)} broadcast(bf16[256,8,16]{0,2,1:T(8,128)(2,1)S(1)} %pad_maximum_fusion.1), dimensions={1,2,3} | broadcast | bytes 2162688 | tf_op jit(solution)/shard_map/broadcast_in_dim | solution.py:20
  39.4 4.3 %all-to-all-start.1 = ((bf16[32,256,8,16]{1,3,2,0:T(8,128)(2,1)}), bf16[32,256,8,16]{1,3,2,0:T(8,128)(2,1)S(1)}, u32[]{:S(2)}, u32[]{:S(2)}) async-start(bf16[32,256,8,16]{1,3,2,0:T(8,128)(2,1)} %broadcast_in_dim.2), calls=%async_computation.1 | async-start | bytes 4194304 | tf_op jit(solution)/shard_map/all_to_all | solution.py:21
  43.8 11.6 %fusion.15 = (f32[8192]{0:T(1024)S(1)}, f32[16,8192]{1,0:T(8,128)S(1)}) fusion(bf16[8192,1536]{1,0:T(8,128)(2,1)} %bitcast.76, bf16[1536,8]{0,1:T(8,128)(2,1)S(1)} %get-tuple-element.10, bf16[1536,8]{0,1:T(8,128)(2,1)S(1)} %get-tuple-element.9), kind=kOutput, calls=%fused_computation.24 | convolution fusion | flops 403005440 | bytes 25772032 | tf_op jit(solution)/shard_map/dot_general | solution.py:44
  55.7 37.7 %all-to-all-done.1 = bf16[32,256,8,16]{1,3,2,0:T(8,128)(2,1)S(1)} async-done(((bf16[32,256,8,16]{1,3,2,0:T(8,128)(2,1)}), bf16[32,256,8,16]{1,3,2,0:T(8,128)(2,1)S(1)}, u32[]{:S(2)}, u32[]{:S(2)}) %all-to-all-start.1) | async-done | bytes 2097184 | tf_op jit(solution)/shard_map/all_to_all | solution.py:21
  93.4 1.7 %broadcast_multiply_fusion = bf16[256,256,2,8]{0,3,2,1:T(8,128)(2,1)} fusion(bf16[256,256,2,8]{0,3,2,1:T(8,128)(2,1)S(1)} %bitcast.78, bf16[256]{0:T(256)(128)(2,1)S(1)} %convert_element_type.94), kind=kLoop, calls=%fused_computation.22 | loop fusion | flops 1048576 | bytes 4194816 | tf_op jit(solution)/shard_map/mul | solution.py:82
  95.1 3.0 %copy.51 = bf16[256,256,2,8]{1,0,2,3:T(8,128)(2,1)S(1)} copy(bf16[256,256,2,8]{0,3,2,1:T(8,128)(2,1)} %broadcast_multiply_fusion) | data formatting | bytes 4194304 | tf_op jit(solution)/shard_map/mul | solution.py:82
  99.6 0.9 copy.53
  100.5 1.0 reshape.71
  101.5 16.7 %all_to_all.29 = bf16[32,2,2048]{2,1,0:T(2,128)(2,1)S(1)} all-to-all(bf16[32,2,2048]{2,1,0:T(2,128)(2,1)S(1)} %reshape.71), channel_id=1, replica_groups=mesh['grp'=8,'chan'=32] {'chan'}, dimensions={0} | all-to-all | bytes 524288 | tf_op jit(solution)/shard_map/all_to_all | solution.py:114
  118.7 0.8 copy.54
  120.2 1.7 %copy.56 = f32[2,8,8,32,32]{4,3,2,1,0:T(8,128)} copy(f32[2,8,8,32,32]{4,2,3,1,0:T(8,128)S(1)} %bitcast.77) | data formatting | bytes 1048576 | tf_op jit(solution)/shard_map/mul | solution.py:117
  122.0 3.1 %mul.184 = f32[2,8,8,1024]{3,2,1,0:T(8,128)} reshape(f32[2,8,8,32,32]{4,3,2,1,0:T(8,128)} %copy.56) | data formatting | bytes 1048576 | tf_op jit(solution)/shard_map/mul | solution.py:117
  (28 shorter events, 4.9 us)
Async XLA Ops:
  4.8 13.0 %copy-start = (s32[8,256]{1,0:T(8,128)S(1)}, s32[8,256]{1,0:T(8,128)}, u32[]{:S(2)}) copy-start(s32[8,256]{1,0:T(8,128)} %param.7) | copy-start | bytes 24580
  6.5 21.3 %all-to-all-start = ((bf16[32,2,512]{2,1,0:T(2,128)(2,1)}), bf16[32,2,512]{2,1,0:T(2,128)(2,1)S(1)}, u32[]{:S(2)}, u32[]{:S(2)}) async-start(bf16[32,2,512]{2,1,0:T(2,128)(2,1)} %reshape.69), calls=%async_computation | async-start | bytes 131072 | tf_op jit(solution)/shard_map/all_to_all | solution.py:106
  39.4 4.3 %copy-start.1 = (s32[256]{0:T(256)S(1)}, s32[256]{0:T(256)}, u32[]{:S(2)}) copy-start(s32[256]{0:T(256)} %param.9) | copy-start | bytes 3076
  39.4 54.0 %all-to-all-start.1 = ((bf16[32,256,8,16]{1,3,2,0:T(8,128)(2,1)}), bf16[32,256,8,16]{1,3,2,0:T(8,128)(2,1)S(1)}, u32[]{:S(2)}, u32[]{:S(2)}) async-start(bf16[32,256,8,16]{1,3,2,0:T(8,128)(2,1)} %broadcast_in_dim.2), calls=%async_computation.1 | async-start | bytes 4194304 | tf_op jit(solution)/shard_map/all_to_all | solution.py:21
  43.8 11.7 %copy-start.2 = (s32[32]{0:T(128)S(1)}, s32[32]{0:T(128)}, u32[]{:S(2)}) copy-start(s32[32]{0:T(128)} %param.8) | copy-start | bytes 388
where the time goes:
time: 125 us
  waiting for transfers between devices  47.6 us (38%)
  matrix products  26.3 us (21%)
  blocking collectives  16.7 us (13%)
  local copies, waits for them, and re-layouts  16.1 us (13%)
  starting transfers between devices  15.6 us (12%)
  other arithmetic  2.44 us (2%)
    all_to_all x1, waiting for transfers between devices, from_everyone(): return lax.all_to_all(copies, axis, split_axis=0, concat_axis=0, tiled=True)  37.7 us
    dot_general x10, matrix products, matmul(): return jnp.dot(left, right, preferred_element_type=jnp.float32)  24.9 us
    all_to_all x1, blocking collectives, shards(): lax.all_to_all(block_cross.astype(jnp.bfloat16), 'chan', split_axis=2, co...  16.7 us
    all_to_all x1, starting transfers between devices, shards(): lax.all_to_all(outgoing, 'chan', split_axis=1, concat_axis=0, tiled=True)  11.3 us
    all_to_all x1, waiting for transfers between devices, shards(): lax.all_to_all(outgoing, 'chan', split_axis=1, concat_axis=0, tiled=True)  9.95 us
    mul x3, local copies, waits for them, and re-layouts, shards(): return result * (1.0 / math.sqrt(SEG * SAMPLES))  5.38 us
    all_to_all x1, starting transfers between devices, from_everyone(): return lax.all_to_all(copies, axis, split_axis=0, concat_axis=0, tiled=True)  4.32 us
    unnamed x10, local copies, waits for them, and re-layouts  3.11 us
  transfers between devices with their start and end apart: 2, of which 2 were waited for; matrix products, arithmetic and copies ran while one was open for 10% of the time, Pallas kernels for 0%

commit v1 on v0

--- a/solution.py
+++ b/solution.py
@@ -8,6 +8,13 @@
 SAMPLES = 1536
 NFREQ = 8
 FIRST_BIN = 24
+
+
+def stacked_exchange(x, axis, split, join):
+    devices = lax.axis_size(axis)
+    pieces = jnp.stack(jnp.split(x, devices, axis=split), axis=0)
+    pieces = lax.all_to_all(pieces, axis, split_axis=0, concat_axis=0)
+    return jnp.concatenate(pieces, axis=join)
 
 
 def laid_out(blocks, dim):
@@ -111,9 +118,9 @@
     filtered_block = filtered_block.reshape(block_width, seg_local, 2 * NFREQ)
     piece = collect(filtered_block, "chan", 1)
     block_cross = pair_spectra(piece, segment_keep, bands_local)
-    result = lax.all_to_all(
-        block_cross.astype(jnp.bfloat16), "chan", split_axis=2, concat_axis=3, tiled=True
-    ).astype(block_cross.dtype)
+    result = stacked_exchange(block_cross.astype(jnp.bfloat16), "chan", 2, 3).astype(
+        block_cross.dtype
+    )
     return result * (1.0 / math.sqrt(SEG * SAMPLES))
 
 

time: 125 us -> 149 us (1.19)
  local copies, waits for them, and re-layouts: 16.1 us -> 35.9 us
  other arithmetic: 2.44 us -> 5.68 us
    another operation x1 -> x33, local copies, waits for them, and re-layouts: 0.95 us -> 22.8 us  [stacked_exchange(): pieces = jnp.stack(jnp.split(x, devices, axis=split), axis=0)]
    another operation x2 -> x5, other arithmetic: 0.33 us -> 3.36 us  [the longest x4 3.07 us: stacked_exchange(): pieces = jnp.stack(jnp.split(x, devices, axis=split), axis=0)]
    mul x3 -> x2, local copies, waits for them, and re-layouts: 5.38 us -> 2.96 us  [shards(): return result * (1.0 / math.sqrt(SEG * SAMPLES))]
    unnamed x10 -> x67, local copies, waits for them, and re-layouts: 3.11 us -> 4.26 us
  transfers between devices with their start and end apart: 2 -> 2, of which waited for: 2 -> 2; matrix products, arithmetic and copies ran while one was open for 10% -> 8% of each run, Pallas kernels for 0% -> 0%
where the time goes in v1:
time: 149 us; the launch traced here: 148 us
  waiting for transfers between devices  47.6 us (32%)
  local copies, waits for them, and re-layouts  35.9 us (24%)
  matrix products  26.3 us (18%)
  blocking collectives  16.7 us (11%)
  starting transfers between devices  15.6 us (10%)
  other arithmetic  5.68 us (4%)
    all_to_all x1, waiting for transfers between devices, from_everyone(): return lax.all_to_all(copies, axis, split_axis=0, concat_axis=0, tiled=True)  37.7 us
    dot_general x10, matrix products, matmul(): return jnp.dot(left, right, preferred_element_type=jnp.float32)  24.9 us
    another operation x33, local copies, waits for them, and re-layouts, stacked_exchange(): pieces = jnp.stack(jnp.split(x, devices, axis=split), axis=0)  22.8 us
    all_to_all x1, blocking collectives, stacked_exchange(): pieces = lax.all_to_all(pieces, axis, split_axis=0, concat_axis=0)  16.7 us
    all_to_all x1, starting transfers between devices, shards(): lax.all_to_all(outgoing, 'chan', split_axis=1, concat_axis=0, tiled=True)  11.3 us
    all_to_all x1, waiting for transfers between devices, shards(): lax.all_to_all(outgoing, 'chan', split_axis=1, concat_axis=0, tiled=True)  9.95 us
    all_to_all x1, starting transfers between devices, from_everyone(): return lax.all_to_all(copies, axis, split_axis=0, concat_axis=0, tiled=True)  4.32 us
    unnamed x67, local copies, waits for them, and re-layouts  4.26 us
  transfers between devices with their start and end apart: 2, of which 2 were waited for; matrix products, arithmetic and copies ran while one was open for 8% of the time, Pallas kernels for 0%

profile of v1, /device:TPU:16, one launch (start us, length us, event | category | flops | bytes accessed | tf_op | source)
XLA Modules:
  0.0 148.4 jit_solution(17311059230770294558)
XLA Ops:
  0.3 4.5 %fusion = bf16[2048,16]{0,1:T(8,128)(2,1)S(1)} fusion(bf16[2048,1536]{1,0:T(8,128)(2,1)} %bitcast.139, bf16[1536,8]{0,1:T(8,128)(2,1)S(1)} %get-tuple-element.42, bf16[1536,8]{0,1:T(8,128)(2,1)S(1)} %get-tuple-element.41), kind=kOutput, calls=%fused_computation.1 | convolution fusion | flops 100794368 | bytes 6406144 | tf_op jit(solution)/shard_map/dot_general | solution.py:51
  6.5 11.3 %all-to-all-start = ((bf16[32,2,512]{2,1,0:T(2,128)(2,1)}), bf16[32,2,512]{2,1,0:T(2,128)(2,1)S(1)}, u32[]{:S(2)}, u32[]{:S(2)}) async-start(bf16[32,2,512]{2,1,0:T(2,128)(2,1)} %reshape.68), calls=%async_computation | async-start | bytes 131072 | tf_op jit(solution)/shard_map/all_to_all | solution.py:113
  17.8 9.9 %all-to-all-done = bf16[32,2,512]{2,1,0:T(2,128)(2,1)S(1)} async-done(((bf16[32,2,512]{2,1,0:T(2,128)(2,1)}), bf16[32,2,512]{2,1,0:T(2,128)(2,1)S(1)}, u32[]{:S(2)}, u32[]{:S(2)}) %all-to-all-start) | async-done | bytes 65568 | tf_op jit(solution)/shard_map/all_to_all | solution.py:113
  37.8 1.6 %broadcast_in_dim.2 = bf16[32,256,8,16]{1,3,2,0:T(8,128)(2,1)} broadcast(bf16[256,8,16]{0,2,1:T(8,128)(2,1)S(1)} %pad_maximum_fusion.1), dimensions={1,2,3} | broadcast | bytes 2162688 | tf_op jit(solution)/shard_map/broadcast_in_dim | solution.py:27
  39.4 4.3 %all-to-all-start.1 = ((bf16[32,256,8,16]{1,3,2,0:T(8,128)(2,1)}), bf16[32,256,8,16]{1,3,2,0:T(8,128)(2,1)S(1)}, u32[]{:S(2)}, u32[]{:S(2)}) async-start(bf16[32,256,8,16]{1,3,2,0:T(8,128)(2,1)} %broadcast_in_dim.2), calls=%async_computation.1 | async-start | bytes 4194304 | tf_op jit(solution)/shard_map/all_to_all | solution.py:28
  43.7 11.6 %fusion.15 = (f32[8192]{0:T(1024)S(1)}, f32[16,8192]{1,0:T(8,128)S(1)}) fusion(bf16[8192,1536]{1,0:T(8,128)(2,1)} %bitcast.137, bf16[1536,8]{0,1:T(8,128)(2,1)S(1)} %get-tuple-element.42, bf16[1536,8]{0,1:T(8,128)(2,1)S(1)} %get-tuple-element.41), kind=kOutput, calls=%fused_computation.87 | convolution fusion | flops 403005440 | bytes 25772032 | tf_op jit(solution)/shard_map/dot_general | solution.py:51
  55.7 37.7 %all-to-all-done.1 = bf16[32,256,8,16]{1,3,2,0:T(8,128)(2,1)S(1)} async-done(((bf16[32,256,8,16]{1,3,2,0:T(8,128)(2,1)}), bf16[32,256,8,16]{1,3,2,0:T(8,128)(2,1)S(1)}, u32[]{:S(2)}, u32[]{:S(2)}) %all-to-all-start.1) | async-done | bytes 2097184 | tf_op jit(solution)/shard_map/all_to_all | solution.py:28
  93.4 1.7 %broadcast_multiply_fusion = bf16[256,256,2,8]{0,3,2,1:T(8,128)(2,1)} fusion(bf16[256,256,2,8]{0,3,2,1:T(8,128)(2,1)S(1)} %bitcast.138, bf16[256]{0:T(256)(128)(2,1)S(1)} %convert_element_type.93), kind=kLoop, calls=%fused_computation.85 | loop fusion | flops 1048576 | bytes 4194816 | tf_op jit(solution)/shard_map/mul | solution.py:89
  95.1 3.0 %copy.61 = bf16[256,256,2,8]{1,0,2,3:T(8,128)(2,1)S(1)} copy(bf16[256,256,2,8]{0,3,2,1:T(8,128)(2,1)} %broadcast_multiply_fusion) | data formatting | bytes 4194304 | tf_op jit(solution)/shard_map/mul | solution.py:89
  99.5 1.3 fusion.88
  104.1 1.6 %copy.64 = bf16[1,2,8,8,32]{4,3,2,1,0:T(8,128)(2,1)} copy(bf16[1,2,8,8,32]{3,4,2,1,0:T(8,128)(2,1)} %get-tuple-element.9) | data formatting | bytes 16384 | tf_op jit(solution)/shard_map/stack | solution.py:15
  105.7 1.6 %copy.65 = bf16[1,2,8,8,32]{4,3,2,1,0:T(8,128)(2,1)} copy(bf16[1,2,8,8,32]{3,4,2,1,0:T(8,128)(2,1)} %get-tuple-element.10) | data formatting | bytes 16384 | tf_op jit(solution)/shard_map/stack | solution.py:15
  107.3 1.6 %copy.66 = bf16[1,2,8,8,32]{4,3,2,1,0:T(8,128)(2,1)} copy(bf16[1,2,8,8,32]{3,4,2,1,0:T(8,128)(2,1)} %get-tuple-element.11) | data formatting | bytes 16384 | tf_op jit(solution)/shard_map/stack | solution.py:15
  108.9 1.6 %copy.67 = bf16[1,2,8,8,32]{4,3,2,1,0:T(8,128)(2,1)} copy(bf16[1,2,8,8,32]{3,4,2,1,0:T(8,128)(2,1)} %get-tuple-element.12) | data formatting | bytes 16384 | tf_op jit(solution)/shard_map/stack | solution.py:15
  110.5 1.6 %copy.68 = bf16[1,2,8,8,32]{4,3,2,1,0:T(8,128)(2,1)} copy(bf16[1,2,8,8,32]{3,4,2,1,0:T(8,128)(2,1)} %get-tuple-element.13) | data formatting | bytes 16384 | tf_op jit(solution)/shard_map/stack | solution.py:15
  112.1 1.6 %copy.69 = bf16[1,2,8,8,32]{4,3,2,1,0:T(8,128)(2,1)} copy(bf16[1,2,8,8,32]{3,4,2,1,0:T(8,128)(2,1)} %get-tuple-element.14) | data formatting | bytes 16384 | tf_op jit(solution)/shard_map/stack | solution.py:15
  113.8 1.6 %copy.70 = bf16[1,2,8,8,32]{4,3,2,1,0:T(8,128)(2,1)} copy(bf16[1,2,8,8,32]{3,4,2,1,0:T(8,128)(2,1)} %get-tuple-element.15) | data formatting | bytes 16384 | tf_op jit(solution)/shard_map/stack | solution.py:15
  115.4 1.6 %copy.71 = bf16[1,2,8,8,32]{4,3,2,1,0:T(8,128)(2,1)} copy(bf16[1,2,8,8,32]{3,4,2,1,0:T(8,128)(2,1)} %get-tuple-element.17) | data formatting | bytes 16384 | tf_op jit(solution)/shard_map/stack | solution.py:15
  117.0 1.6 %copy.72 = bf16[1,2,8,8,32]{4,3,2,1,0:T(8,128)(2,1)} copy(bf16[1,2,8,8,32]{3,4,2,1,0:T(8,128)(2,1)} %get-tuple-element.18) | data formatting | bytes 16384 | tf_op jit(solution)/shard_map/stack | solution.py:15
  118.6 1.6 %copy.73 = bf16[1,2,8,8,32]{4,3,2,1,0:T(8,128)(2,1)} copy(bf16[1,2,8,8,32]{3,4,2,1,0:T(8,128)(2,1)} %get-tuple-element.19) | data formatting | bytes 16384 | tf_op jit(solution)/shard_map/stack | solution.py:15
  120.2 1.6 %copy.74 = bf16[1,2,8,8,32]{4,3,2,1,0:T(8,128)(2,1)} copy(bf16[1,2,8,8,32]{3,4,2,1,0:T(8,128)(2,1)} %get-tuple-element.20) | data formatting | bytes 16384 | tf_op jit(solution)/shard_map/stack | solution.py:15
  121.8 1.6 %copy.75 = bf16[1,2,8,8,32]{4,3,2,1,0:T(8,128)(2,1)} copy(bf16[1,2,8,8,32]{3,4,2,1,0:T(8,128)(2,1)} %get-tuple-element.21) | data formatting | bytes 16384 | tf_op jit(solution)/shard_map/stack | solution.py:15
  128.0 16.7 %all_to_all.25 = bf16[32,2,2048]{2,1,0:T(2,128)(2,1)S(1)} all-to-all(bf16[32,2,2048]{2,1,0:T(2,128)(2,1)S(1)} %reshape.70), channel_id=1, replica_groups=mesh['grp'=8,'chan'=32] {'chan'}, dimensions={0} | all-to-all | bytes 524288 | tf_op jit(solution)/shard_map/all_to_all | solution.py:16
  146.7 1.7 %mul.180 = f32[2,8,8,1024]{3,2,1,0:T(8,128)} reshape(f32[2,8,8,32,32]{4,3,2,1,0:T(8,128)S(1)} %copy.95) | data formatting | bytes 1048576 | tf_op jit(solution)/shard_map/mul | solution.py:124
  (118 shorter events, 23.2 us)
Async XLA Ops:
  4.8 13.0 %copy-start.13 = (s32[8,256]{1,0:T(8,128)S(1)}, s32[8,256]{1,0:T(8,128)}, u32[]{:S(2)}) copy-start(s32[8,256]{1,0:T(8,128)} %param.7) | copy-start | bytes 24580
  6.5 21.3 %all-to-all-start = ((bf16[32,2,512]{2,1,0:T(2,128)(2,1)}), bf16[32,2,512]{2,1,0:T(2,128)(2,1)S(1)}, u32[]{:S(2)}, u32[]{:S(2)}) async-start(bf16[32,2,512]{2,1,0:T(2,128)(2,1)} %reshape.68), calls=%async_computation | async-start | bytes 131072 | tf_op jit(solution)/shard_map/all_to_all | solution.py:113
  39.4 4.3 %copy-start.14 = (s32[256]{0:T(256)S(1)}, s32[256]{0:T(256)}, u32[]{:S(2)}) copy-start(s32[256]{0:T(256)} %param.9) | copy-start | bytes 3076
  39.4 54.0 %all-to-all-start.1 = ((bf16[32,256,8,16]{1,3,2,0:T(8,128)(2,1)}), bf16[32,256,8,16]{1,3,2,0:T(8,128)(2,1)S(1)}, u32[]{:S(2)}, u32[]{:S(2)}) async-start(bf16[32,256,8,16]{1,3,2,0:T(8,128)(2,1)} %broadcast_in_dim.2), calls=%async_computation.1 | async-start | bytes 4194304 | tf_op jit(solution)/shard_map/all_to_all | solution.py:28
  43.7 11.7 %copy-start.15 = (s32[32]{0:T(128)S(1)}, s32[32]{0:T(128)}, u32[]{:S(2)}) copy-start(s32[32]{0:T(128)} %param.8) | copy-start | bytes 388
  124.2 2.5 %copy-start.2 = (bf16[1,2,8,8,32]{4,3,2,1,0:T(8,128)(2,1)S(1)}, bf16[1,2,8,8,32]{4,3,2,1,0:T(8,128)(2,1)}, u32[]{:S(2)}) copy-start(bf16[1,2,8,8,32]{4,3,2,1,0:T(8,128)(2,1)} %copy.74) | copy-start | bytes 24580
  124.2 2.5 %copy-start.1 = (bf16[1,2,8,8,32]{4,3,2,1,0:T(8,128)(2,1)S(1)}, bf16[1,2,8,8,32]{4,3,2,1,0:T(8,128)(2,1)}, u32[]{:S(2)}) copy-start(bf16[1,2,8,8,32]{4,3,2,1,0:T(8,128)(2,1)} %copy.75) | copy-start | bytes 24580
  124.2 2.5 %copy-start = (bf16[1,2,8,8,32]{4,3,2,1,0:T(8,128)(2,1)S(1)}, bf16[1,2,8,8,32]{4,3,2,1,0:T(8,128)(2,1)}, u32[]{:S(2)}) copy-start(bf16[1,2,8,8,32]{4,3,2,1,0:T(8,128)(2,1)} %copy.76) | copy-start | bytes 24580
  124.3 2.3 %copy-start.5 = (bf16[1,2,8,8,32]{4,3,2,1,0:T(8,128)(2,1)S(1)}, bf16[1,2,8,8,32]{4,3,2,1,0:T(8,128)(2,1)}, u32[]{:S(2)}) copy-start(bf16[1,2,8,8,32]{4,3,2,1,0:T(8,128)(2,1)} %copy.71) | copy-start | bytes 24580
  124.3 2.3 %copy-start.4 = (bf16[1,2,8,8,32]{4,3,2,1,0:T(8,128)(2,1)S(1)}, bf16[1,2,8,8,32]{4,3,2,1,0:T(8,128)(2,1)}, u32[]{:S(2)}) copy-start(bf16[1,2,8,8,32]{4,3,2,1,0:T(8,128)(2,1)} %copy.72) | copy-start | bytes 24580
  124.3 2.3 %copy-start.3 = (bf16[1,2,8,8,32]{4,3,2,1,0:T(8,128)(2,1)S(1)}, bf16[1,2,8,8,32]{4,3,2,1,0:T(8,128)(2,1)}, u32[]{:S(2)}) copy-start(bf16[1,2,8,8,32]{4,3,2,1,0:T(8,128)(2,1)} %copy.73) | copy-start | bytes 24580
  124.4 2.1 %copy-start.8 = (bf16[1,2,8,8,32]{4,3,2,1,0:T(8,128)(2,1)S(1)}, bf16[1,2,8,8,32]{4,3,2,1,0:T(8,128)(2,1)}, u32[]{:S(2)}) copy-start(bf16[1,2,8,8,32]{4,3,2,1,0:T(8,128)(2,1)} %copy.68) | copy-start | bytes 24580
  124.4 2.1 %copy-start.7 = (bf16[1,2,8,8,32]{4,3,2,1,0:T(8,128)(2,1)S(1)}, bf16[1,2,8,8,32]{4,3,2,1,0:T(8,128)(2,1)}, u32[]{:S(2)}) copy-start(bf16[1,2,8,8,32]{4,3,2,1,0:T(8,128)(2,1)} %copy.69) | copy-start | bytes 24580
  124.4 2.1 %copy-start.6 = (bf16[1,2,8,8,32]{4,3,2,1,0:T(8,128)(2,1)S(1)}, bf16[1,2,8,8,32]{4,3,2,1,0:T(8,128)(2,1)}, u32[]{:S(2)}) copy-start(bf16[1,2,8,8,32]{4,3,2,1,0:T(8,128)(2,1)} %copy.70) | copy-start | bytes 24580
  124.6 1.8 %copy-start.11 = (bf16[1,2,8,8,32]{4,3,2,1,0:T(8,128)(2,1)S(1)}, bf16[1,2,8,8,32]{4,3,2,1,0:T(8,128)(2,1)}, u32[]{:S(2)}) copy-start(bf16[1,2,8,8,32]{4,3,2,1,0:T(8,128)(2,1)} %copy.64) | copy-start | bytes 24580
  124.6 1.8 %copy-start.10 = (bf16[1,2,8,8,32]{4,3,2,1,0:T(8,128)(2,1)S(1)}, bf16[1,2,8,8,32]{4,3,2,1,0:T(8,128)(2,1)}, u32[]{:S(2)}) copy-start(bf16[1,2,8,8,32]{4,3,2,1,0:T(8,128)(2,1)} %copy.66) | copy-start | bytes 24580
  124.6 1.9 %copy-start.9 = (bf16[1,2,8,8,32]{4,3,2,1,0:T(8,128)(2,1)S(1)}, bf16[1,2,8,8,32]{4,3,2,1,0:T(8,128)(2,1)}, u32[]{:S(2)}) copy-start(bf16[1,2,8,8,32]{4,3,2,1,0:T(8,128)(2,1)} %copy.67) | copy-start | bytes 24580
  124.7 1.7 %copy-start.12 = (bf16[1,2,8,8,32]{4,3,2,1,0:T(8,128)(2,1)S(1)}, bf16[1,2,8,8,32]{4,3,2,1,0:T(8,128)(2,1)}, u32[]{:S(2)}) copy-start(bf16[1,2,8,8,32]{4,3,2,1,0:T(8,128)(2,1)} %copy.65) | copy-start | bytes 24580
